TPU v7x, 32 devices: a whole 2x2x4 slice. The times are simulated.
32 devices in a mesh: blk: 8 (over z, x), ga: 4 (over y, core).
Axes of the slice: x: 2, y: 2, z: 4, core: 2. Of those that a mesh axis runs over, the one named last changes fastest.
Arguments:
- pair_val: bfloat16 [16, 16, 16, 2048], P('blk', None, None, 'ga'), may hold values from -0.125 to 0.125
- pair_con: bfloat16 [16, 16, 16, 2048], P('blk', None, None, 'ga'), may hold values from -6 to 6
- screened: bfloat16 [16, 2048, 2048], P('blk', None, 'ga'), may hold values from -0.125 to 0.125
- amplitude: bfloat16 [16, 16], P('blk'), may hold values from -6 to 6
- qmap: int32 [16, 16], P('blk'), may hold values from 0 to 15, as said below
Outputs:
- kernel_x: float32 [16, 16], P('blk')
Inputs may be any that keep to these rules, and one draw needn't show every extreme that they name: qmap[k, k'] is the label of the difference k - k' (periodic) on a grid of 8 by 2 points, with the points and the differences labelled at random; every row and every column holds each label once.
All inputs are finite; a program needn't handle non-finite values.
Results may differ from a plain program's by a relative error of at most 0.004.
Values may be sent and summed in bfloat16 or wider, within the bound.
No kernel may reach another device: no remote copies, remote signals or barrier semaphores. Data moves between devices by JAX's collectives and lax.ppermute only.
A program may use at most 64 MiB of HBM per device.

v0:
```python
import jax
import jax.numpy as jnp
from jax import lax
from jax.sharding import PartitionSpec as P

NV = 4
NC = 4


def inverse_rows(qmap):
    total = qmap.shape[1]
    labels = jnp.arange(total, dtype=jnp.int32)
    hits = (qmap[:, :, None] == labels[None, None, :]).astype(jnp.int32)
    return jnp.sum(hits * labels[None, :, None], axis=1)


def kernel_unit(sent_con, screened):
    summed = jnp.einsum(
        "kqxg,qgh->kqxh",
        lax.all_gather(sent_con, "ga", axis=3, tiled=True),
        screened,
        preferred_element_type=jnp.float32,
    )
    return summed.astype(jnp.bfloat16)


def contract(unit, zeta):
    count, labels, width = (unit.shape[0], unit.shape[1], unit.shape[3])
    unit_five = unit.reshape(count, labels, NC, NC, width)
    zeta_five = zeta.reshape(count, labels, NV, NC, width)
    terms = jnp.einsum(
        "nqcyg,nqayg->nqac", unit_five, zeta_five, preferred_element_type=jnp.float32
    )
    return terms.reshape(count, labels, NV * NC)


def body(pair_val, pair_con, screened, amplitude, qmap):
    local_k, total, band_pairs, width = pair_val.shape
    every_amp = lax.all_gather(amplitude, "blk", axis=0, tiled=True)
    partner = inverse_rows(qmap)
    val_sorted = jnp.take_along_axis(pair_val, partner[:, :, None, None], axis=1)
    con_sorted = jnp.take_along_axis(pair_con, partner[:, :, None, None], axis=1)
    amp_sorted = every_amp[partner].reshape(local_k, total, NV, NC)
    val_five = val_sorted.reshape(local_k, total, NV, NV, width)
    zeta = jnp.einsum("kqavg,kqvc->kqacg", val_five, amp_sorted, preferred_element_type=jnp.float32)
    zeta = zeta.astype(jnp.bfloat16).reshape(local_k, total, NV * NC, width)
    sent_zeta, sent_con = (
        lax.all_to_all(zeta, "blk", split_axis=1, concat_axis=0, tiled=True),
        lax.all_to_all(con_sorted, "blk", split_axis=1, concat_axis=0, tiled=True),
    )
    unit = kernel_unit(sent_con, screened)
    partial_value = contract(unit, sent_zeta)
    back = lax.all_to_all(partial_value, "blk", split_axis=0, concat_axis=1, tiled=True)
    summed = jnp.sum(back, 1)
    result = lax.psum(summed, "ga")
    return result / total


def solution(mesh):
    placed = (
        P("blk", None, None, "ga"),
        P("blk", None, None, "ga"),
        P("blk", None, "ga"),
        P("blk", None),
        P("blk", None),
    )
    return jax.shard_map(
        body, mesh=mesh, in_specs=placed, out_specs=P("blk", None), check_vma=False
    )
```

profile of v0, /device:TPU:0, one launch (start us, length us, event | category | flops | bytes accessed | tf_op | source)
XLA Modules:
  0.0 94.8 jit_solution(7691314893441121280)
XLA Ops:
  6.5 0.0 copy-start
  6.5 0.0 copy-start.1
  6.5 0.0 all-gather.3.cloned.1.call-start
  6.5 0.8 select_reduce_fusion
  7.4 0.1 reshape.94
  7.5 0.1 copy-done
  7.6 0.6 gather_fusion.2
  8.2 1.7 %gather_fusion.1 = bf16[32,16,512]{2,1,0:T(8,128)(2,1)S(1)} fusion(bf16[2,16,16,512]{3,2,1,0:T(8,128)(2,1)} %param.7, s32[32]{0:T(128)S(1)} %reshape.94), kind=kCustom, calls=%fused_computation.clone | custom fusion | bytes 1048832 | tf_op jit(solution)/shard_map/jit(take_along_axis)/gather | solution.py:41
  9.9 0.2 broadcast_select_fusion.1
  10.1 21.6 %all_to_all.42 = bf16[2,16,16,512]{3,2,0,1:T(8,128)(2,1)S(1)} all-to-all(bf16[2,16,16,512]{3,2,0,1:T(8,128)(2,1)S(1)} %copy.53), channel_id=1, replica_groups=mesh['blk'=8,'ga'=4] {'blk'}, dimensions={1} | all-to-all | bytes 1048576 | tf_op jit(solution)/shard_map/all_to_all | solution.py:49
  31.7 0.8 copy.55
  32.5 0.0 all-gather.3.cloned.1.call-update
  32.6 0.1 reshape.73
  32.7 0.0 copy-done.1
  32.7 18.6 %all-gather = bf16[8,2,16]{2,1,0:T(2,128)(2,1)S(1)} all-gather(bf16[1,2,16]{2,1,0:T(2,128)(2,1)S(1)} %bitcast.70), channel_id=1, replica_groups=mesh['blk'=8,'ga'=4] {'blk'}, dimensions={0}, use_global_device_ids=true | all-gather | bytes 576 | tf_op jit(solution)/shard_map/all_gather | solution.py:39
  51.2 0.6 gather_fusion
  51.8 0.1 copy.48
  51.9 0.1 reshape.52
  52.0 0.1 copy.62
  52.1 0.1 reshape.53
  52.3 0.4 fusion.5
  52.7 0.1 reshape.54
  52.9 13.1 %all_to_all.43 = bf16[2,16,16,512]{3,2,0,1:T(8,128)(2,1)S(1)} all-to-all(bf16[2,16,16,512]{3,2,0,1:T(8,128)(2,1)S(1)} %copy.50), channel_id=1, replica_groups=mesh['blk'=8,'ga'=4] {'blk'}, dimensions={1} | all-to-all | bytes 1048576 | tf_op jit(solution)/shard_map/all_to_all | solution.py:48
  65.9 0.5 copy.52
  66.5 0.0 all-gather.3.cloned.1.call-done
  66.5 4.1 %fusion.6 = bf16[16,2,16,512]{3,2,0,1:T(8,128)(2,1)S(1)} fusion(bf16[16,2,16,2048]{3,2,0,1:T(8,128)(2,1)} %all-gather.3.cloned.1.call-done, bf16[2,2048,512]{2,1,0:T(8,128)(2,1)} %param.9), kind=kOutput, calls=%fused_computation.8 | convolution fusion | flops 1074003968 | bytes 6815744 | tf_op jit(solution)/shard_map/kqxg,qgh->kqxh/dot_general | solution.py:18
  70.6 0.1 reshape.56
  70.7 0.8 convolution_bitcast_fusion
  71.5 0.1 copy.58
  71.6 0.1 copy.59
  71.7 10.0 %all_to_all.44 = f32[16,2,16]{2,1,0:T(2,128)S(1)} all-to-all(f32[16,2,16]{2,1,0:T(2,128)S(1)} %copy.59), channel_id=1, replica_groups=mesh['blk'=8,'ga'=4] {'blk'}, dimensions={0} | all-to-all | bytes 4096 | tf_op jit(solution)/shard_map/all_to_all | solution.py:53
  81.8 5.7 %psum.7 = f32[2,16]{1,0:T(2,128)S(1)} all-reduce(f32[2,16]{1,0:T(2,128)S(1)} %reduce_sum.31), channel_id=1, replica_groups=mesh['blk'=8,'ga'=4] {'ga'}, use_global_device_ids=true, to_apply=%region_3.0 | all-reduce | flops 32 | bytes 256 | tf_op jit(solution)/shard_map/psum | solution.py:55
  87.4 0.6 broadcast_multiply_fusion
  (7 shorter events, 0.1 us)
Async XLA Ops:
  6.5 1.1 %copy-start = (bf16[2,16,16,512]{3,2,1,0:T(8,128)(2,1)S(1)}, bf16[2,16,16,512]{3,2,1,0:T(8,128)(2,1)}, u32[]{:S(2)}) copy-start(bf16[2,16,16,512]{3,2,1,0:T(8,128)(2,1)} %param.8) | copy-start | bytes 1572868
  6.5 26.1 %copy-start.1 = (bf16[2,16]{1,0:T(2,128)(2,1)S(1)}, bf16[2,16]{1,0:T(2,128)(2,1)}, u32[]{:S(2)}) copy-start(bf16[2,16]{1,0:T(2,128)(2,1)} %param.10) | copy-start | bytes 196
  6.5 60.0 %all-gather.3.cloned.1.call-start = ((), (), s32[]{:S(2)}) async-start(), calls=%async_computation.3 | async-start | bytes 2621440 | tf_op jit(solution)/shard_map/all_gather | solution.py:20
Sparse Core Ops, SparseCore 0:
  32.7 21.5 all-gather.2
where the time goes:
time: 95.2 us; the launch traced here: 94.8 us
  blocking collectives  68.9 us (72%)
  between operations  13.5 us (14%)
  local copies, waits for them, and re-layouts  5.52 us (6%)
  matrix products  5.27 us (6%)
  other arithmetic  1.62 us (2%)
    all_to_all x1, blocking collectives, body(): lax.all_to_all(con_sorted, 'blk', split_axis=1, concat_axis=0, tiled=True)  21.6 us
    all_gather x1, blocking collectives, body(): every_amp = lax.all_gather(amplitude, 'blk', axis=0, tiled=True)  18.6 us
    all_to_all x1, blocking collectives, body(): lax.all_to_all(zeta, 'blk', split_axis=1, concat_axis=0, tiled=True)  13.1 us
    all_to_all x1, blocking collectives, body(): lax.all_to_all(partial_value, 'blk', split_axis=0, concat_axis=1, tiled=T...  10 us
    psum x1, blocking collectives, body(): result = lax.psum(summed, 'ga')  5.66 us
    dot_general x1, matrix products, kernel_unit(): jnp.einsum('kqxg,qgh->kqxh', lax.all_gather(sent_con, 'ga', axis=3, tiled...  4.07 us
  transfers between devices with their start and end apart: 1, of which 0 were waited for; matrix products, arithmetic and copies ran while one was open for 2% of the time, Pallas kernels for 0%

commit v1 on v0

v1 whole, which is shorter than its diff:
```python
import jax
import jax.numpy as jnp
from jax import lax
from jax.sharding import PartitionSpec as P

NV = 4
NC = 4


def inverse_rows(qmap):
    total = qmap.shape[1]
    labels = jnp.arange(total, dtype=jnp.int32)
    hits = (qmap[:, :, None] == labels[None, None, :]).astype(jnp.int32)
    return jnp.sum(hits * labels[None, :, None], axis=1)


def swap(value, axis, size, step):
    return lax.ppermute(value, axis, [(i, i ^ step) for i in range(size)])


def body_of(blk, ga):
    def body(pair_val, pair_con, screened, amplitude, qmap):
        local_k, total, band_pairs, width = pair_val.shape
        local_q = screened.shape[0]
        slot = lax.axis_index("ga")
        every_amp = lax.all_gather(amplitude, "blk", axis=0, tiled=True)
        partner = inverse_rows(qmap)
        con_sorted = jnp.take_along_axis(pair_con, partner[:, :, None, None], axis=1)
        con_sorted, every_amp = lax.optimization_barrier((con_sorted, every_amp))
        con_in = lax.all_to_all(con_sorted, "blk", split_axis=1, concat_axis=0, tiled=True)

        val_sorted = jnp.take_along_axis(pair_val, partner[:, :, None, None], axis=1)
        amp_sorted = every_amp[partner].reshape(local_k, total, NV, NC)
        val_five = val_sorted.reshape(local_k, total, NV, NV, width)
        zeta = jnp.einsum("kqavg,kqvc->kqacg", val_five, amp_sorted, preferred_element_type=jnp.float32)
        zeta = zeta.astype(jnp.bfloat16).reshape(local_k, total, NV * NC, width)

        far = swap(con_in, "ga", ga, ga // 2)
        near = swap(con_in, "ga", ga, 1)
        zeta_in = lax.all_to_all(zeta, "blk", split_axis=1, concat_axis=0, tiled=True)
        pieces = {0: con_in, 1: near, ga // 2: far, ga // 2 + 1: swap(far, "ga", ga, 1)}
        weights = screened.reshape(local_q, ga, width, screened.shape[2])
        unit = 0.0
        for key, held in pieces.items():
            block = lax.dynamic_index_in_dim(weights, slot ^ key, 1, keepdims=False)
            unit = unit + jnp.einsum("kqxg,qgh->kqxh", held, block,
                                     preferred_element_type=jnp.float32)
        unit = unit.astype(jnp.bfloat16).reshape(total, local_q, NC, NC, -1)
        zeta = zeta_in.reshape(total, local_q, NV, NC, -1)
        terms = jnp.einsum("kqcyg,kqayg->kac", unit, zeta, preferred_element_type=jnp.float32)
        terms = terms.reshape(blk, 1, local_k, NV * NC)
        terms = jnp.broadcast_to(terms, (blk, ga, local_k, NV * NC)).reshape(blk * ga, local_k, NV * NC)
        back = lax.all_to_all(terms, ("blk", "ga"), split_axis=0, concat_axis=0, tiled=True)
        return jnp.sum(back, 0) / total
    return body


def solution(mesh):
    placed = (
        P("blk", None, None, "ga"),
        P("blk", None, None, "ga"),
        P("blk", None, "ga"),
        P("blk", None),
        P("blk", None),
    )
    return jax.shard_map(
        body_of(mesh.shape["blk"], mesh.shape["ga"]), mesh=mesh, in_specs=placed,
        out_specs=P("blk", None), check_vma=False
    )
```

time: 95.2 us -> 75.1 us (0.79)
  blocking collectives: 68.9 us -> 33.2 us
  waiting for transfers between devices: 0.04 us -> 19.6 us
  between operations: 13.5 us -> 0.19 us
  starting transfers between devices: 0.01 us -> 8.84 us
  local copies, waits for them, and re-layouts: 5.52 us -> 6.81 us
    all_to_all x3 -> x1, blocking collectives: 44.7 us -> 10.8 us  [body(): lax.all_to_all(terms, ('blk', 'ga'), split_axis=0, concat_axis=0, tiled=T...]
    all_to_all x0 -> x2, waiting for transfers between devices: none -> 19.2 us  [the longest x1 10.8 us: body(): lax.all_to_all(zeta, 'blk', split_axis=1, concat_axis=0, tiled=True)]
    all_to_all x0 -> x2, starting transfers between devices: none -> 7.18 us  [the longest x1 3.69 us: body(): lax.all_to_all(zeta, 'blk', split_axis=1, concat_axis=0, tiled=True)]
    psum x1 -> x0, blocking collectives: 5.66 us -> none  [body(): result = lax.psum(summed, 'ga')]
    all_gather x1, blocking collectives: 18.6 us -> 22.4 us  [body(): every_amp = lax.all_gather(amplitude, 'blk', axis=0, tiled=True)]
    ppermute x0 -> x3, starting transfers between devices: none -> 1.66 us  [swap(): return lax.ppermute(value, axis, [(i, i ^ step) for i in range(size)])]
    gather x2 -> x1, local copies, waits for them, and re-layouts: 1.75 us -> 0.62 us  [body(): jnp.take_along_axis(pair_val, partner[:, :, None, None], axis=1)]
    gather x1 -> x2, local copies, waits for them, and re-layouts: 0.62 us -> 1.75 us  [body(): jnp.take_along_axis(pair_con, partner[:, :, None, None], axis=1)]
  transfers between devices with their start and end apart: 1 -> 5, of which waited for: 0 -> 3; matrix products, arithmetic and copies ran while one was open for 2% -> 8% of each run, Pallas kernels for 0% -> 0%
where the time goes in v1:
time: 75.1 us; the launch traced here: 74.7 us
  blocking collectives  33.2 us (44%)
  waiting for transfers between devices  19.6 us (26%)
  starting transfers between devices  8.84 us (12%)
  local copies, waits for them, and re-layouts  6.81 us (9%)
  matrix products  4.45 us (6%)
  other arithmetic  1.62 us (2%)
    all_gather x1, blocking collectives, body(): every_amp = lax.all_gather(amplitude, 'blk', axis=0, tiled=True)  22.4 us
    all_to_all x1, waiting for transfers between devices, body(): lax.all_to_all(zeta, 'blk', split_axis=1, concat_axis=0, tiled=True)  10.8 us
    all_to_all x1, blocking collectives, body(): lax.all_to_all(terms, ('blk', 'ga'), split_axis=0, concat_axis=0, tiled=T...  10.8 us
    all_to_all x1, waiting for transfers between devices, body(): lax.all_to_all(con_sorted, 'blk', split_axis=1, concat_axis=0, tiled=True)  8.4 us
    all_to_all x1, starting transfers between devices, body(): lax.all_to_all(zeta, 'blk', split_axis=1, concat_axis=0, tiled=True)  3.69 us
    all_to_all x1, starting transfers between devices, body(): lax.all_to_all(con_sorted, 'blk', split_axis=1, concat_axis=0, tiled=True)  3.49 us
    dot_general x4, matrix products, body(): jnp.einsum('kqxg,qgh->kqxh', held, block, preferred_element_type=jnp.floa...  3.15 us
    gather x2, local copies, waits for them, and re-layouts, body(): jnp.take_along_axis(pair_con, partner[:, :, None, None], axis=1)  1.75 us
  transfers between devices with their start and end apart: 5, of which 3 were waited for; matrix products, arithmetic and copies ran while one was open for 8% of the time, Pallas kernels for 0%

profile of v1, /device:TPU:0, one launch (start us, length us, event | category | flops | bytes accessed | tf_op | source)
XLA Modules:
  0.0 74.7 jit_solution(2706167675406388047)
XLA Ops:
  0.0 0.0 copy-start
  0.0 0.8 %select_reduce_fusion = s32[2,16]{1,0:T(2,128)S(1)} fusion(s32[2,16]{1,0:T(2,128)} %param.11), kind=kLoop, calls=%fused_computation.24 | loop fusion | flops 1504 | bytes 256 | tf_op jit(solution)/shard_map/reduce_sum | solution.py:14
  0.9 0.1 reshape.99
  0.9 0.1 copy-done
  1.1 0.6 gather_fusion.2
  1.7 1.7 %gather_fusion.1 = bf16[32,16,512]{2,1,0:T(8,128)(2,1)S(1)} fusion(bf16[2,16,16,512]{3,2,1,0:T(8,128)(2,1)} %param.8, s32[32]{0:T(128)S(1)} %reshape.99), kind=kCustom, calls=%fused_computation.clone | custom fusion | bytes 1048832 | tf_op jit(solution)/shard_map/jit(take_along_axis)/gather | solution.py:28
  3.4 22.4 %all-gather = bf16[8,2,16]{2,1,0:T(2,128)(2,1)S(1)} all-gather(bf16[1,2,16]{2,1,0:T(2,128)(2,1)} %bitcast.98), channel_id=1, replica_groups=mesh['blk'=8,'ga'=4] {'blk'}, dimensions={0}, use_global_device_ids=true | all-gather | bytes 576 | tf_op jit(solution)/shard_map/all_gather | solution.py:26
  25.8 0.2 broadcast_select_fusion
  26.0 0.8 %copy.96 = bf16[2,16,16,512]{3,2,0,1:T(8,128)(2,1)} copy(bf16[2,16,16,512]{3,2,1,0:T(8,128)(2,1)S(1)} %get-tuple-element.9) | data formatting | bytes 1048576 | tf_op jit(solution)/shard_map/optimization_barrier | solution.py:29
  26.8 3.5 %all-to-all-start.1 = ((bf16[2,16,16,512]{3,2,0,1:T(8,128)(2,1)}), bf16[2,16,16,512]{3,2,0,1:T(8,128)(2,1)S(1)}, u32[]{:S(2)}, u32[]{:S(2)}) async-start(bf16[2,16,16,512]{3,2,0,1:T(8,128)(2,1)} %copy.96), calls=%async_computation.1 | async-start | bytes 1048576 | tf_op jit(solution)/shard_map/all_to_all | solution.py:30
  30.3 0.1 reshape.78
  30.4 0.6 gather_fusion
  31.0 0.1 copy.90
  31.1 0.1 reshape.56
  31.1 0.1 copy.107
  31.3 0.1 reshape.57
  31.4 0.4 fusion.2
  31.8 0.1 reshape.58
  32.0 0.8 %copy.92 = bf16[2,16,16,512]{3,2,0,1:T(8,128)(2,1)} copy(bf16[2,16,16,512]{3,2,1,0:T(8,128)(2,1)S(1)} %reshape.58) | data formatting | bytes 1048576 | tf_op jit(solution)/shard_map/reshape | solution.py:36
  32.8 8.4 %all-to-all-done.1 = bf16[2,16,16,512]{3,2,0,1:T(8,128)(2,1)S(1)} async-done(((bf16[2,16,16,512]{3,2,0,1:T(8,128)(2,1)}), bf16[2,16,16,512]{3,2,0,1:T(8,128)(2,1)S(1)}, u32[]{:S(2)}, u32[]{:S(2)}) %all-to-all-start.1) | async-done | bytes 524320 | tf_op jit(solution)/shard_map/all_to_all | solution.py:30
  41.2 3.7 %all-to-all-start = ((bf16[2,16,16,512]{3,2,0,1:T(8,128)(2,1)}), bf16[2,16,16,512]{3,2,0,1:T(8,128)(2,1)S(1)}, u32[]{:S(2)}, u32[]{:S(2)}) async-start(bf16[2,16,16,512]{3,2,0,1:T(8,128)(2,1)} %copy.92), calls=%async_computation | async-start | bytes 1048576 | tf_op jit(solution)/shard_map/all_to_all | solution.py:40
  45.0 1.6 %collective-permute-start.1 = (bf16[16,2,16,512]{3,2,0,1:T(8,128)(2,1)S(1)}, bf16[16,2,16,512]{3,2,0,1:T(8,128)(2,1)S(1)}, u32[]{:S(2)}, u32[]{:S(2)}) collective-permute-start(bf16[16,2,16,512]{3,2,0,1:T(8,128)(2,1)S(1)} %bitcast.92), channel_id=1, source_target_pairs={{0,2},{1,3},{2,0},{3,1},{4,6},{5,7},{6,4},{7,5},{8,10},{9,11},{10,... | collective-permute-start | bytes 1572872 | tf_op jit(solution)/shard_map/ppermute | solution.py:18
  46.5 0.0 collective-permute-start
  46.5 10.8 %all-to-all-done = bf16[2,16,16,512]{3,2,0,1:T(8,128)(2,1)S(1)} async-done(((bf16[2,16,16,512]{3,2,0,1:T(8,128)(2,1)}), bf16[2,16,16,512]{3,2,0,1:T(8,128)(2,1)S(1)}, u32[]{:S(2)}, u32[]{:S(2)}) %all-to-all-start) | async-done | bytes 524320 | tf_op jit(solution)/shard_map/all_to_all | solution.py:40
  57.3 0.5 copy.94
  57.9 0.0 copy-start.1
  57.9 1.8 %fusion.6 = f32[2,512,16,16]{1,3,2,0:T(8,128)S(1)} fusion(bf16[16,2,16,512]{3,2,0,1:T(8,128)(2,1)S(1)} %bitcast.94, bf16[2,4,512,512]{3,2,1,0:T(8,128)(2,1)} %bitcast.99, s32[]{:T(128)S(6)} %select_n.30), kind=kOutput, calls=%fused_computation.14 | convolution fusion | flops 268435456 | bytes 2621444 | tf_op jit(solution)/shard_map/kqxg,qgh->kqxh/dot_general | solution.py:46
  59.7 0.0 collective-permute-done.1
  59.7 0.1 collective-permute-start.2
  59.8 0.0 collective-permute-done
  59.8 0.6 copy-done.1
  60.4 0.4 convolution_add_fusion.2
  60.9 0.5 convolution_add_fusion.1
  61.3 0.4 collective-permute-done.2
  61.7 0.4 fusion.1
  62.2 0.1 reshape.61
  62.3 0.9 %convolution_bitcast_fusion = f32[16,4,4]{2,1,0:T(4,128)S(1)} fusion(bf16[16,2,4,4,512]{4,3,2,0,1:T(4,128)(2,1)S(1)} %reshape.61, bf16[16,2,4,4,512]{4,1,3,2,0:T(2,128)(2,1)S(1)} %bitcast.95), kind=kOutput, calls=%fused_computation.10 | convolution fusion | flops 2097152 | bytes 1049600 | tf_op jit(solution)/shard_map/kqcyg,kqayg->kac/dot_general | solution.py:50
  63.2 0.1 broadcast_in_dim.22
  63.3 10.8 %all_to_all.38 = f32[32,2,16]{2,1,0:T(2,128)S(1)} all-to-all(f32[32,2,16]{2,1,0:T(2,128)S(1)} %copy.105), channel_id=1, replica_groups=mesh['blk'=8,'ga'=4] {'blk','ga'}, dimensions={0} | all-to-all | bytes 8192 | tf_op jit(solution)/shard_map/all_to_all | solution.py:53
  74.2 0.6 broadcast_multiply_fusion
  (8 shorter events, 0.1 us)
Async XLA Ops:
  0.0 1.1 %copy-start = (bf16[2,16,16,512]{3,2,1,0:T(8,128)(2,1)S(1)}, bf16[2,16,16,512]{3,2,1,0:T(8,128)(2,1)}, u32[]{:S(2)}) copy-start(bf16[2,16,16,512]{3,2,1,0:T(8,128)(2,1)} %param.7) | copy-start | bytes 1572868
  26.8 14.4 %all-to-all-start.1 = ((bf16[2,16,16,512]{3,2,0,1:T(8,128)(2,1)}), bf16[2,16,16,512]{3,2,0,1:T(8,128)(2,1)S(1)}, u32[]{:S(2)}, u32[]{:S(2)}) async-start(bf16[2,16,16,512]{3,2,0,1:T(8,128)(2,1)} %copy.96), calls=%async_computation.1 | async-start | bytes 1048576 | tf_op jit(solution)/shard_map/all_to_all | solution.py:30
  41.2 16.1 %all-to-all-start = ((bf16[2,16,16,512]{3,2,0,1:T(8,128)(2,1)}), bf16[2,16,16,512]{3,2,0,1:T(8,128)(2,1)S(1)}, u32[]{:S(2)}, u32[]{:S(2)}) async-start(bf16[2,16,16,512]{3,2,0,1:T(8,128)(2,1)} %copy.92), calls=%async_computation | async-start | bytes 1048576 | tf_op jit(solution)/shard_map/all_to_all | solution.py:40
  45.0 14.8 %collective-permute-start.1 = (bf16[16,2,16,512]{3,2,0,1:T(8,128)(2,1)S(1)}, bf16[16,2,16,512]{3,2,0,1:T(8,128)(2,1)S(1)}, u32[]{:S(2)}, u32[]{:S(2)}) collective-permute-start(bf16[16,2,16,512]{3,2,0,1:T(8,128)(2,1)S(1)} %bitcast.92), channel_id=1, source_target_pairs={{0,2},{1,3},{2,0},{3,1},{4,6},{5,7},{6,4},{7,5},{8,10},{9,11},{10,... | collective-permute-start | bytes 1572872 | tf_op jit(solution)/shard_map/ppermute | solution.py:18
  46.5 13.3 %collective-permute-start = (bf16[16,2,16,512]{3,2,0,1:T(8,128)(2,1)S(1)}, bf16[16,2,16,512]{3,2,0,1:T(8,128)(2,1)S(1)}, u32[]{:S(2)}, u32[]{:S(2)}) collective-permute-start(bf16[16,2,16,512]{3,2,0,1:T(8,128)(2,1)S(1)} %bitcast.93), channel_id=1, source_target_pairs={{0,1},{1,0},{2,3},{3,2},{4,5},{5,4},{6,7},{7,6},{8,9},{9,8},{10,11... | collective-permute-start | bytes 1572872 | tf_op jit(solution)/shard_map/ppermute | solution.py:18
  57.9 2.5 %copy-start.1 = (bf16[2,2048,512]{2,1,0:T(8,128)(2,1)S(1)}, bf16[2,2048,512]{2,1,0:T(8,128)(2,1)}, u32[]{:S(2)}) copy-start(bf16[2,2048,512]{2,1,0:T(8,128)(2,1)} %param.9) | copy-start | bytes 12582916
  59.7 2.0 %collective-permute-start.2 = (bf16[16,2,16,512]{3,2,0,1:T(8,128)(2,1)S(1)}, bf16[16,2,16,512]{3,2,0,1:T(8,128)(2,1)S(1)}, u32[]{:S(2)}, u32[]{:S(2)}) collective-permute-start(bf16[16,2,16,512]{3,2,0,1:T(8,128)(2,1)S(1)} %collective-permute-done.1), channel_id=1, source_target_pairs={{0,1},{1,0},{2,3},{3,2},{4,5},{5,4},{6,7},{7,6},{8,9},{9,8},{10,11... | collective-permute-start | bytes 1572872 | tf_op jit(solution)/shard_map/ppermute | solution.py:18
